TPU v7x, 128 devices: a whole 4x4x4 slice. The times are simulated.
128 devices in a mesh: gx: 4 (over z), gy: 4 (over y), gz: 8 (over x, core).
Axes of the slice: x: 4, y: 4, z: 4, core: 2. Of those that a mesh axis runs over, the one named last changes fastest.
Arguments:
- fields: float32 [40, 32, 64, 1024], P(None, 'gx', 'gy', 'gz'), may hold values from 0.1 to 1.5
- source: float32 [40, 32, 64, 1024], P(None, 'gx', 'gy', 'gz'), may hold values from 0.005 to 0.2
- velocity: float32 [3, 32, 64, 1024], P(None, 'gx', 'gy', 'gz'), may hold values from -1 to 1
- diffusivity: float32 [40], replicated, may hold values from 0.02 to 0.09
- reacting: int32 [32, 64, 8], P('gx', 'gy', 'gz'), may hold values from 0 to 1, as said below
- counts: int32 [32, 64, 8], P('gx', 'gy', 'gz'), may hold values from 1 to 4
- mechanism: int32 [4, 100], replicated, may hold values from 0 to 21
- prefactor: float32 [100], replicated, may hold values from 0.5 to 5
- activation: float32 [100], replicated, may hold values from 0.3 to 3
- heat_release: float32 [100], replicated, may hold values from 0.01 to 0.1
Outputs:
- evolved: float32 [40, 32, 64, 1024], P(None, 'gx', 'gy', 'gz')
Inputs may be any that keep to these rules, and one draw needn't show every extreme that they name: `reacting`: over all devices exactly 2048 blocks react, and on one device all of its 128 blocks react.
All inputs are finite; a program needn't handle non-finite values.
Results may differ from a plain program's by a relative error of at most 0.0003.
Values sent between devices are 32-bit elements; how exact they have to be, the bound alone decides.
No kernel may reach another device: no remote copies, remote signals or barrier semaphores. Data moves between devices by JAX's collectives and lax.ppermute only.
A program may use at most 128 MiB of HBM per device.

v0:
```python
import jax
import jax.numpy as jnp
from jax import lax
from jax.sharding import Mesh
from jax.sharding import PartitionSpec as P

SPECIES = 22
REACTIONS = 100
CZ = 128
SUB = 4
GZ = ("gz_0", "gz_1")
GX_GY_GZ = ("gx", "gy", "gz_0", "gz_1")


courant = 0.15
chem_step = 0.25


def extended(array, sides, width):
    edges = {}
    for axis, dim in sides:
        size, length = (lax.axis_size(axis), array.shape[dim])
        up = [(i, (i + 1) % size) for i in range(size - 1)]
        last = lax.slice_in_dim(array, length - width, length, axis=dim)
        initial = lax.slice_in_dim(array, 0, width, axis=dim)
        edges[dim] = (
            lax.ppermute(last, axis, up),
            lax.ppermute(initial, axis, [(b, a) for a, b in up]),
        )
    done = []
    for _, dim in sides:
        low, high = edges[dim]
        around = [(width, width) if d in done else (0, 0) for d in range(array.ndim)]
        array = jnp.concatenate([jnp.pad(low, around), array, jnp.pad(high, around)], axis=dim)
        done.append(dim)
    return array


def passed_along(value, axis, steps):
    count = lax.axis_size(axis)
    initial, last = (max(0, -steps), min(count, count - steps))
    return lax.ppermute(value, axis, [(source, source + steps) for source in range(initial, last)])


def nothing_yet(array, identity):
    return jnp.zeros_like(array) + jnp.asarray(identity, array.dtype)


def entering(array, axes, combine, identity):
    before = start = nothing_yet(array, identity)
    total = array
    for axis in reversed(axes):
        length, position = (lax.axis_size(axis), lax.axis_index(axis))
        pieces = lax.all_gather(total, axis)
        inside, total = (start, start)
        for k in range(length):
            passed = k < position
            total = combine(total, pieces[k])
            inside = jnp.where(passed, total, inside)
        before = combine(inside, before)
    return before


def advance(fields, velocity, diffusivity, source):
    padded = extended(fields, (("gx", 1), ("gy", 2)), 1)
    below_face = passed_along(fields[:, :, :, -1:], GZ, 1)
    above_face = passed_along(fields[:, :, :, :1], GZ, -1)
    depth = fields.shape[3]
    lane = lax.broadcasted_iota(jnp.int32, (1, 1, 1, depth), 3)
    down_z = jnp.where(lane == 0, below_face, jnp.roll(fields, 1, axis=3))
    up_z = jnp.where(lane == depth - 1, above_face, jnp.roll(fields, -1, axis=3))
    up_cells = (padded[:, 2:, 1:-1, :], padded[:, 1:-1, 2:, :], up_z)
    down_cells = (padded[:, :-2, 1:-1, :], padded[:, 1:-1, :-2, :], down_z)
    diffuse = diffusivity[:, None, None, None]
    result = fields + source
    for direction in range(3):
        flow_speed = velocity[direction][None]
        result = result - courant * (
            jnp.maximum(flow_speed, 0.0) * (fields - down_cells[direction])
            + jnp.minimum(flow_speed, 0.0) * (up_cells[direction] - fields)
        )
        result = result + diffuse * (up_cells[direction] + down_cells[direction] - 2.0 * fields)
    return result


def react(chem_state, sub_counts, mechanism, prefactor, activation, heat_release):
    species_row = lax.broadcasted_iota(jnp.int32, (1, SPECIES), 1)
    species_col = lax.broadcasted_iota(jnp.int32, (SPECIES, 1), 0)
    reactant_ids = mechanism[0:2].reshape(-1)
    takers = (reactant_ids[:, None] == species_row).astype(jnp.float32)
    losers = jnp.transpose(takers)
    makers = (mechanism[2][None, :] == species_col).astype(jnp.float32) + (
        mechanism[3][None, :] == species_col
    ).astype(jnp.float32)
    makers = jnp.concatenate([makers, heat_release[None, :]], 0)
    interval = chem_step / sub_counts.astype(jnp.float32)
    for substep in range(SUB):
        fractions = chem_state[:SPECIES]
        temper = chem_state[SPECIES]
        rate_const = prefactor[:, None, None] * jnp.exp(-activation[:, None, None] / temper[None])
        paired = jnp.take(fractions, reactant_ids, axis=0)
        reactant_one = paired[:REACTIONS]
        reactant_two = paired[REACTIONS:]
        progress = rate_const * reactant_one * reactant_two
        loss_rate = jnp.einsum(
            "kj,jnc->knc",
            losers,
            jnp.concatenate([rate_const * reactant_two, rate_const * reactant_one], 0),
            precision=lax.Precision.HIGHEST,
        )
        gain_rate = jnp.einsum("kj,jnc->knc", makers, progress, precision=lax.Precision.HIGHEST)
        widths = interval[None, :, None]
        renewed_fractions = (fractions + widths * gain_rate[:SPECIES]) / (1.0 + widths * loss_rate)
        renewed_temper = temper + interval[:, None] * gain_rate[SPECIES]
        renewed = jnp.concatenate([renewed_fractions, renewed_temper[None]], 0)
        chem_state = jnp.where((substep < sub_counts)[None, :, None], renewed, chem_state)
    return chem_state


def add_counts(earlier, later):
    return earlier + later


def body(
    fields,
    source,
    velocity,
    diffusivity,
    reacting,
    counts,
    mechanism,
    prefactor,
    activation,
    heat_release,
):
    current = advance(fields, velocity, diffusivity, source)
    current = advance(current, velocity, diffusivity, source)
    rows_x = current.shape[1]
    rows_y = current.shape[2]
    block_count = rows_x * rows_y
    chem_state = current[: SPECIES + 1].reshape(SPECIES + 1, block_count, CZ)
    marked = reacting.reshape(block_count)
    sub_counts = counts.reshape(block_count)
    peer_count = lax.axis_size(GX_GY_GZ)
    slot_count = -(-block_count // peer_count)
    total_slots = peer_count * slot_count
    live_mask = (marked == 1).astype(jnp.int32)
    own_total = jnp.sum(live_mask)
    offset = entering(own_total, GX_GY_GZ, add_counts, jnp.int32(0))
    local_rank = jnp.cumsum(live_mask) - live_mask
    target = (offset + local_rank + peer_count // 2) % peer_count
    position = jnp.where(
        live_mask == 1, target * slot_count + local_rank // peer_count, total_slots
    )
    outgoing = (
        jnp.zeros((SPECIES + 1, total_slots, CZ), jnp.float32)
        .at[:, position]
        .set(chem_state, mode="drop")
    )
    out_counts = jnp.zeros((1, total_slots), jnp.int32).at[0, position].set(sub_counts, mode="drop")
    incoming, in_counts = (
        lax.all_to_all(outgoing, GX_GY_GZ, split_axis=1, concat_axis=1, tiled=True),
        lax.all_to_all(out_counts, GX_GY_GZ, split_axis=1, concat_axis=1, tiled=True),
    )
    capacity = max(2, block_count // 8)
    arrived = in_counts[0] > 0
    picked = jnp.nonzero(arrived, size=capacity, fill_value=total_slots)[0]
    gathered = jnp.take(incoming, picked, axis=1, mode="clip")
    work_counts = jnp.where(picked < total_slots, jnp.take(in_counts[0], picked, mode="clip"), 1)
    reacted = react(gathered, work_counts, mechanism, prefactor, activation, heat_release)
    replies = incoming.at[:, picked].set(reacted, mode="drop")
    returned = lax.all_to_all(replies, GX_GY_GZ, split_axis=1, concat_axis=1, tiled=True)
    homebound = jnp.take(returned, position, axis=1, mode="clip")
    renewed = jnp.where((live_mask == 1)[None, :, None], homebound, chem_state)
    return jnp.concatenate(
        [renewed.reshape(SPECIES + 1, rows_x, rows_y, CZ), current[SPECIES + 1 :]], 0
    )


def solution(mesh):
    torus = Mesh(
        mesh.devices.reshape(mesh.shape["gx"], mesh.shape["gy"], 4, 2), ("gx", "gy", "gz_0", "gz_1")
    )
    placed = (
        P(None, "gx", "gy", GZ),
        P(None, "gx", "gy", GZ),
        P(None, "gx", "gy", GZ),
        P(),
        P("gx", "gy", GZ),
        P("gx", "gy", GZ),
        P(),
        P(),
        P(),
        P(),
    )
    return jax.shard_map(
        body, mesh=torus, in_specs=placed, out_specs=P(None, "gx", "gy", GZ), check_vma=False
    )
```

profile of v0, /device:TPU:1, one launch (start us, length us, event | category | flops | bytes accessed | tf_op | source)
XLA Modules:
  0.0 268.5 jit_solution(6778746690111591574)
XLA Ops:
  0.0 2.0 fusion.155
  2.0 4.4 %collective-permute-start = (f32[40,1,16,128]{3,2,1,0:T(8,128)}, f32[40,1,16,128]{3,2,1,0:T(8,128)S(1)}, u32[]{:S(2)}, u32[]{:S(2)}) collective-permute-start(f32[40,1,16,128]{3,2,1,0:T(8,128)} %get-tuple-element.27), channel_id=1, source_target_pairs={{0,32},{32,64},{64,96},{1,33},{33,65},{65,97},{2,34},{34,66},{66,9... | collective-permute-start | bytes 983048 | tf_op jit(solution)/shard_map/ppermute | solution.py:27
  7.7 5.8 %fusion.153 = (f32[40,8,16,1]{3,2,1,0:T(8,128)}, f32[40,8,16,1]{3,2,1,0:T(8,128)}) fusion(f32[40,8,16,128]{3,2,1,0:T(8,128)} %param.12), kind=kLoop, calls=%fused_computation.240 | loop fusion | bytes 81920 | tf_op jit(solution)/shard_map/slice | solution.py:66
  13.5 3.7 %copy.326 = f32[40,8,16,1]{0,2,3,1:T(8,128)} copy(f32[40,8,16,1]{3,2,1,0:T(8,128)} %get-tuple-element.23) | data formatting | bytes 40960 | tf_op jit(solution)/shard_map/slice | solution.py:66
  17.3 3.9 %collective-permute-start.4 = (f32[40,8,16,1]{0,2,3,1:T(8,128)}, f32[40,8,16,1]{0,2,3,1:T(8,128)}, u32[]{:S(2)}, u32[]{:S(2)}) collective-permute-start(f32[40,8,16,1]{0,2,3,1:T(8,128)} %copy.326), channel_id=1, source_target_pairs={{0,1},{1,2},{2,3},{3,4},{4,5},{5,6},{6,7},{8,9},{9,10},{10,11},{11... | collective-permute-start | bytes 61448 | tf_op jit(solution)/shard_map/ppermute | solution.py:42
  21.2 3.6 %copy.328 = f32[40,8,16,1]{0,2,3,1:T(8,128)} copy(f32[40,8,16,1]{3,2,1,0:T(8,128)} %get-tuple-element.24) | data formatting | bytes 40960 | tf_op jit(solution)/shard_map/slice | solution.py:67
  24.8 1.9 collective-permute-start.5
  27.7 3.9 %collective-permute-start.2 = (f32[40,8,1,128]{3,2,1,0:T(1,128)}, f32[40,8,1,128]{3,2,1,0:T(1,128)}, u32[]{:S(2)}, u32[]{:S(2)}) collective-permute-start(f32[40,8,1,128]{3,2,1,0:T(1,128)} %get-tuple-element.21), channel_id=1, source_target_pairs={{0,8},{8,16},{16,24},{1,9},{9,17},{17,25},{2,10},{10,18},{18,26},{... | collective-permute-start | bytes 491528 | tf_op jit(solution)/shard_map/ppermute | solution.py:27
  39.5 7.4 %all-reduce.6 = s32[4]{0:T(128)S(1)} all-reduce(s32[4]{0:T(128)S(1)} %dynamic-update-slice.1), channel_id=1, replica_groups=mesh['gx'=4,'gy'=4,'gz_0'=4,'gz_1'=2] {'gz_0'}, use_global_device_ids=true, to_apply=%add.6 | all-reduce | flops 4 | bytes 32
  51.6 6.1 %all-reduce.7 = s32[4]{0:T(128)S(1)} all-reduce(s32[4]{0:T(128)S(1)} %dynamic-update-slice.2), channel_id=1, replica_groups=mesh['gx'=4,'gy'=4,'gz_0'=4,'gz_1'=2] {'gy'}, use_global_device_ids=true, to_apply=%add.7 | all-reduce | flops 4 | bytes 32
  62.5 8.4 %all-reduce.8 = s32[4]{0:T(128)S(1)} all-reduce(s32[4]{0:T(128)S(1)} %dynamic-update-slice.3), channel_id=1, replica_groups=mesh['gx'=4,'gy'=4,'gz_0'=4,'gz_1'=2] {'gx'}, use_global_device_ids=true, to_apply=%add.8 | all-reduce | flops 4 | bytes 32
  80.0 10.8 %all-to-all-start.1 = ((s32[1,128,1]{2,0,1:T(1,128)}), s32[1,128,1]{2,0,1:T(1,128)}, u32[]{:S(2)}, u32[]{:S(2)}) async-start(s32[1,128,1]{2,0,1:T(1,128)} %copy.335), calls=%async_computation.1 | async-start | bytes 131072 | tf_op jit(solution)/shard_map/all_to_all | solution.py:163
  90.9 3.3 %fusion.154 = (f32[40,8,16,127]{3,2,1,0:T(8,128)}, f32[40,8,16,127]{3,2,1,0:T(8,128)}) fusion(f32[40,8,16,128]{3,2,1,0:T(8,128)S(1)} %copy-done), kind=kLoop, calls=%fused_computation.241 | loop fusion | bytes 10403840 | tf_op jit(solution)/shard_map/jit(_roll_static)/slice | solution.py:70
  99.4 2.3 collective-permute-done.3
  101.8 8.8 %fusion.25 = f32[40,8,16,128]{3,2,1,0:T(8,128)S(1)} fusion(f32[40,1,16,128]{3,2,1,0:T(8,128)S(1)} %collective-permute-done.1, f32[40,8,16,128]{3,2,1,0:T(8,128)S(1)} %copy-done.1, f32[40,1,16,128]{3,2,1,0:T(8,128)S(1)} %collective-permute-done, f32[40,8,16,1]{3,2,1,0:T(8,128)} %get-tuple-element.24, f32[40,8,16,127]{3,2,1,0:T(8,128)} %get-tuple-element.26, ...), kind=kLoop, calls=%fused_computation.51 | loop fusion | flops 32112640 | bytes 17801632 | tf_op jit(solution)/shard_map/add | solution.py:82
  110.6 3.3 %fusion.149 = (f32[40,8,16,1]{3,2,1,0:T(8,128)}, f32[40,8,16,1]{3,2,1,0:T(8,128)}) fusion(f32[40,8,16,128]{3,2,1,0:T(8,128)S(1)} %fusion.25), kind=kLoop, calls=%fused_computation.236 | loop fusion | bytes 81920 | tf_op jit(solution)/shard_map/slice | solution.py:66
  114.9 3.0 %copy.330 = f32[40,8,16,1]{0,2,3,1:T(8,128)S(1)} copy(f32[40,8,16,1]{3,2,1,0:T(8,128)} %get-tuple-element.15) | data formatting | bytes 40960 | tf_op jit(solution)/shard_map/slice | solution.py:66
  117.9 5.5 %collective-permute-start.10 = (f32[40,8,16,1]{0,2,3,1:T(8,128)S(1)}, f32[40,8,16,1]{0,2,3,1:T(8,128)S(1)}, u32[]{:S(2)}, u32[]{:S(2)}) collective-permute-start(f32[40,8,16,1]{0,2,3,1:T(8,128)S(1)} %copy.330), channel_id=1, source_target_pairs={{0,1},{1,2},{2,3},{3,4},{4,5},{5,6},{6,7},{8,9},{9,10},{10,11},{11... | collective-permute-start | bytes 61448 | tf_op jit(solution)/shard_map/ppermute | solution.py:42
  124.4 3.6 %copy.332 = f32[40,8,16,1]{0,2,3,1:T(8,128)} copy(f32[40,8,16,1]{3,2,1,0:T(8,128)} %get-tuple-element.16) | data formatting | bytes 40960 | tf_op jit(solution)/shard_map/slice | solution.py:67
  129.9 4.1 %collective-permute-start.6 = (f32[40,1,16,128]{3,2,1,0:T(8,128)}, f32[40,1,16,128]{3,2,1,0:T(8,128)}, u32[]{:S(2)}, u32[]{:S(2)}) collective-permute-start(f32[40,1,16,128]{3,2,1,0:T(8,128)} %get-tuple-element.19), channel_id=1, source_target_pairs={{0,32},{32,64},{64,96},{1,33},{33,65},{65,97},{2,34},{34,66},{66,9... | collective-permute-start | bytes 983048 | tf_op jit(solution)/shard_map/ppermute | solution.py:27
  135.3 3.2 %collective-permute-start.8 = (f32[40,8,1,128]{3,2,1,0:T(1,128)}, f32[40,8,1,128]{3,2,1,0:T(1,128)S(1)}, u32[]{:S(2)}, u32[]{:S(2)}) collective-permute-start(f32[40,8,1,128]{3,2,1,0:T(1,128)} %get-tuple-element.13), channel_id=1, source_target_pairs={{0,8},{8,16},{16,24},{1,9},{9,17},{17,25},{2,10},{10,18},{18,26},{... | collective-permute-start | bytes 491528 | tf_op jit(solution)/shard_map/ppermute | solution.py:27
  139.9 3.3 %fusion.150 = (f32[40,8,16,127]{3,2,1,0:T(8,128)}, f32[40,8,16,127]{3,2,1,0:T(8,128)}) fusion(f32[40,8,16,128]{3,2,1,0:T(8,128)S(1)} %fusion.25), kind=kLoop, calls=%fused_computation.237 | loop fusion | bytes 10403840 | tf_op jit(solution)/shard_map/jit(_roll_static)/slice | solution.py:70
  145.5 9.5 %fusion.10 = f32[40,8,16,128]{3,2,1,0:T(8,128)S(1)} fusion(f32[40,1,16,128]{3,2,1,0:T(8,128)} %collective-permute-done.7, f32[40,8,16,128]{3,2,1,0:T(8,128)S(1)} %fusion.25, f32[40,1,16,128]{3,2,1,0:T(8,128)} %collective-permute-done.6, f32[40,8,16,1]{3,2,1,0:T(8,128)} %get-tuple-element.16, f32[40,8,16,127]{3,2,1,0:T(8,128)} %get-tuple-element.18, ...), kind=kLoop, calls=%fused_computation.28 | loop fusion | flops 34734080 | bytes 14524832 | tf_op jit(solution)/shard_map/add | solution.py:82
  157.7 14.2 %scatter_fusion = f32[23,128,128]{2,0,1:T(8,128)} fusion(f32[23,128,128]{2,0,1:T(8,128)} %broadcast_in_dim.157, s32[128]{0:T(128)S(1)} %get-tuple-element.7, f32[128,23,128]{2,1,0:T(8,128)S(1)} %copy.334), kind=kCustom, calls=%fused_computation.7 | custom fusion | bytes 4522496 | tf_op jit(solution)/shard_map/scatter | solution.py:158
  171.9 15.4 %all-to-all-start = ((f32[23,128,128]{2,0,1:T(8,128)}), f32[23,128,128]{2,0,1:T(8,128)}, u32[]{:S(2)}, u32[]{:S(2)}) async-start(f32[23,128,128]{2,0,1:T(8,128)} %scatter_fusion), calls=%async_computation | async-start | bytes 3145728 | tf_op jit(solution)/shard_map/all_to_all | solution.py:162
  190.1 3.2 %reduce.3 = s32[128]{0:T(128)S(1)} reduce(s32[1,128,1]{2,0,1:T(1,128)} %all-to-all-done.1, s32[]{:T(128)} %constant.112.clone.1), dimensions={0,2}, to_apply=%all_to_all.14.reduce_sub_computation | reduce | bytes 1028 | tf_op jit(solution)/shard_map/all_to_all | solution.py:163
  195.9 15.9 %all-to-all-done = f32[23,128,128]{2,0,1:T(8,128)} async-done(((f32[23,128,128]{2,0,1:T(8,128)}), f32[23,128,128]{2,0,1:T(8,128)}, u32[]{:S(2)}, u32[]{:S(2)}) %all-to-all-start) | async-done | bytes 1507360 | tf_op jit(solution)/shard_map/all_to_all | solution.py:162
  211.9 2.0 gather_fusion.1
  228.2 2.4 scatter_fusion.1
  230.6 5.4 %all-to-all-start.2 = ((f32[23,128,128]{2,0,1:T(8,128)}), f32[23,128,128]{2,0,1:T(8,128)}, u32[]{:S(2)}, u32[]{:S(2)}) async-start(f32[23,128,128]{2,0,1:T(8,128)} %scatter_fusion.1), calls=%async_computation.2 | async-start | bytes 3145728 | tf_op jit(solution)/shard_map/all_to_all | solution.py:172
  236.0 24.7 %all-to-all-done.2 = f32[23,128,128]{2,0,1:T(8,128)} async-done(((f32[23,128,128]{2,0,1:T(8,128)}), f32[23,128,128]{2,0,1:T(8,128)}, u32[]{:S(2)}, u32[]{:S(2)}) %all-to-all-start.2) | async-done | bytes 1507360 | tf_op jit(solution)/shard_map/all_to_all | solution.py:172
  260.7 3.2 %gather_fusion.2 = f32[128,23,128]{2,1,0:T(8,128)} fusion(f32[23,128,128]{2,0,1:T(8,128)} %all-to-all-done.2, s32[1024]{0:T(1024)S(1)} %pad_clamp_fusion), kind=kCustom, calls=%fused_computation.6 | custom fusion | bytes 3015168 | tf_op jit(solution)/shard_map/jit(_take)/gather | solution.py:173
  (182 shorter events, 57.8 us)
Async XLA Ops:
  2.0 96.9 %collective-permute-start = (f32[40,1,16,128]{3,2,1,0:T(8,128)}, f32[40,1,16,128]{3,2,1,0:T(8,128)S(1)}, u32[]{:S(2)}, u32[]{:S(2)}) collective-permute-start(f32[40,1,16,128]{3,2,1,0:T(8,128)} %get-tuple-element.27), channel_id=1, source_target_pairs={{0,32},{32,64},{64,96},{1,33},{33,65},{65,97},{2,34},{34,66},{66,9... | collective-permute-start | bytes 983048 | tf_op jit(solution)/shard_map/ppermute | solution.py:27
  6.4 93.0 %collective-permute-start.1 = (f32[40,1,16,128]{3,2,1,0:T(8,128)}, f32[40,1,16,128]{3,2,1,0:T(8,128)S(1)}, u32[]{:S(2)}, u32[]{:S(2)}) collective-permute-start(f32[40,1,16,128]{3,2,1,0:T(8,128)} %get-tuple-element.28), channel_id=1, source_target_pairs={{32,0},{64,32},{96,64},{33,1},{65,33},{97,65},{34,2},{66,34},{98,6... | collective-permute-start | bytes 983048 | tf_op jit(solution)/shard_map/ppermute | solution.py:28
  13.5 13.2 %copy-start = (f32[40,8,16,128]{3,2,1,0:T(8,128)S(1)}, f32[40,8,16,128]{3,2,1,0:T(8,128)}, u32[]{:S(2)}) copy-start(f32[40,8,16,128]{3,2,1,0:T(8,128)} %param.12) | copy-start | bytes 7864324
  13.5 18.1 %copy-start.18 = (s32[8,16,1]{1,2,0:T(1,128)S(1)}, s32[8,16,1]{1,2,0:T(1,128)}, u32[]{:S(2)}) copy-start(s32[8,16,1]{1,2,0:T(1,128)} %param.16) | copy-start | bytes 1540
  13.5 18.8 %copy-start.28 = (u32[128]{0:T(128)S(1)}, u32[128]{0:T(128)}, u32[]{:S(2)}) copy-start(u32[128]{0:T(128)} %constant.142) | copy-start | bytes 1540
  13.5 23.3 %copy-start.27 = (u32[128]{0:T(128)S(1)}, u32[128]{0:T(128)}, u32[]{:S(2)}) copy-start(u32[128]{0:T(128)} %constant.147) | copy-start | bytes 1540
  13.5 34.1 %copy-start.26 = (u32[128]{0:T(128)S(1)}, u32[128]{0:T(128)}, u32[]{:S(2)}) copy-start(u32[128]{0:T(128)} %constant.152) | copy-start | bytes 1540
  13.5 44.9 %copy-start.25 = (u32[128]{0:T(128)S(1)}, u32[128]{0:T(128)}, u32[]{:S(2)}) copy-start(u32[128]{0:T(128)} %constant.157) | copy-start | bytes 1540
  13.5 58.7 %copy-start.21 = (s32[8,16,1]{1,2,0:T(1,128)S(1)}, s32[8,16,1]{1,2,0:T(1,128)}, u32[]{:S(2)}) copy-start(s32[8,16,1]{1,2,0:T(1,128)} %param.17) | copy-start | bytes 1540
  17.3 77.8 %collective-permute-start.4 = (f32[40,8,16,1]{0,2,3,1:T(8,128)}, f32[40,8,16,1]{0,2,3,1:T(8,128)}, u32[]{:S(2)}, u32[]{:S(2)}) collective-permute-start(f32[40,8,16,1]{0,2,3,1:T(8,128)} %copy.326), channel_id=1, source_target_pairs={{0,1},{1,2},{2,3},{3,4},{4,5},{5,6},{6,7},{8,9},{9,10},{10,11},{11... | collective-permute-start | bytes 61448 | tf_op jit(solution)/shard_map/ppermute | solution.py:42
  24.8 72.5 %collective-permute-start.5 = (f32[40,8,16,1]{0,2,3,1:T(8,128)}, f32[40,8,16,1]{0,2,3,1:T(8,128)}, u32[]{:S(2)}, u32[]{:S(2)}) collective-permute-start(f32[40,8,16,1]{0,2,3,1:T(8,128)} %copy.328), channel_id=1, source_target_pairs={{1,0},{2,1},{3,2},{4,3},{5,4},{6,5},{7,6},{9,8},{10,9},{11,10},{12... | collective-permute-start | bytes 61448 | tf_op jit(solution)/shard_map/ppermute | solution.py:42
  27.7 71.7 %collective-permute-start.2 = (f32[40,8,1,128]{3,2,1,0:T(1,128)}, f32[40,8,1,128]{3,2,1,0:T(1,128)}, u32[]{:S(2)}, u32[]{:S(2)}) collective-permute-start(f32[40,8,1,128]{3,2,1,0:T(1,128)} %get-tuple-element.21), channel_id=1, source_target_pairs={{0,8},{8,16},{16,24},{1,9},{9,17},{17,25},{2,10},{10,18},{18,26},{... | collective-permute-start | bytes 491528 | tf_op jit(solution)/shard_map/ppermute | solution.py:27
  80.0 91.9 %all-to-all-start.1 = ((s32[1,128,1]{2,0,1:T(1,128)}), s32[1,128,1]{2,0,1:T(1,128)}, u32[]{:S(2)}, u32[]{:S(2)}) async-start(s32[1,128,1]{2,0,1:T(1,128)} %copy.335), calls=%async_computation.1 | async-start | bytes 131072 | tf_op jit(solution)/shard_map/all_to_all | solution.py:163
  90.9 3.3 %copy-start.22 = (s32[4,100]{1,0:T(4,128)S(1)}, s32[4,100]{1,0:T(4,128)}, u32[]{:S(2)}) copy-start(s32[4,100]{1,0:T(4,128)} %param.18) | copy-start | bytes 4804
  90.9 3.3 %copy-start.16 = (f32[3,8,16,128]{3,2,1,0:T(8,128)S(1)}, f32[3,8,16,128]{3,2,1,0:T(8,128)}, u32[]{:S(2)}) copy-start(f32[3,8,16,128]{3,2,1,0:T(8,128)} %param.14) | copy-start | bytes 589828
  90.9 4.1 %slice-start.1 = ((s32[4,100]{1,0:T(4,128)}), s32[2,100]{1,0:T(2,128)S(1)}, s32[]{:S(2)}) async-start(s32[4,100]{1,0:T(4,128)} %param.18), calls=%async_computation.4 | async-start | bytes 2048 | tf_op jit(solution)/shard_map/slice | solution.py:89
  95.1 6.7 %collective-permute-start.3 = (f32[40,8,1,128]{3,2,1,0:T(1,128)}, f32[40,8,1,128]{3,2,1,0:T(1,128)}, u32[]{:S(2)}, u32[]{:S(2)}) collective-permute-start(f32[40,8,1,128]{3,2,1,0:T(1,128)} %get-tuple-element.22), channel_id=1, source_target_pairs={{8,0},{16,8},{24,16},{9,1},{17,9},{25,17},{10,2},{18,10},{26,18},{... | collective-permute-start | bytes 491528 | tf_op jit(solution)/shard_map/ppermute | solution.py:28
  117.9 20.6 %collective-permute-start.10 = (f32[40,8,16,1]{0,2,3,1:T(8,128)S(1)}, f32[40,8,16,1]{0,2,3,1:T(8,128)S(1)}, u32[]{:S(2)}, u32[]{:S(2)}) collective-permute-start(f32[40,8,16,1]{0,2,3,1:T(8,128)S(1)} %copy.330), channel_id=1, source_target_pairs={{0,1},{1,2},{2,3},{3,4},{4,5},{5,6},{6,7},{8,9},{9,10},{10,11},{11... | collective-permute-start | bytes 61448 | tf_op jit(solution)/shard_map/ppermute | solution.py:42
  127.9 15.4 %collective-permute-start.11 = (f32[40,8,16,1]{0,2,3,1:T(8,128)}, f32[40,8,16,1]{0,2,3,1:T(8,128)S(1)}, u32[]{:S(2)}, u32[]{:S(2)}) collective-permute-start(f32[40,8,16,1]{0,2,3,1:T(8,128)} %copy.332), channel_id=1, source_target_pairs={{1,0},{2,1},{3,2},{4,3},{5,4},{6,5},{7,6},{9,8},{10,9},{11,10},{12... | collective-permute-start | bytes 61448 | tf_op jit(solution)/shard_map/ppermute | solution.py:42
  129.9 15.6 %collective-permute-start.6 = (f32[40,1,16,128]{3,2,1,0:T(8,128)}, f32[40,1,16,128]{3,2,1,0:T(8,128)}, u32[]{:S(2)}, u32[]{:S(2)}) collective-permute-start(f32[40,1,16,128]{3,2,1,0:T(8,128)} %get-tuple-element.19), channel_id=1, source_target_pairs={{0,32},{32,64},{64,96},{1,33},{33,65},{65,97},{2,34},{34,66},{66,9... | collective-permute-start | bytes 983048 | tf_op jit(solution)/shard_map/ppermute | solution.py:27
  134.0 11.5 %collective-permute-start.7 = (f32[40,1,16,128]{3,2,1,0:T(8,128)}, f32[40,1,16,128]{3,2,1,0:T(8,128)}, u32[]{:S(2)}, u32[]{:S(2)}) collective-permute-start(f32[40,1,16,128]{3,2,1,0:T(8,128)} %get-tuple-element.20), channel_id=1, source_target_pairs={{32,0},{64,32},{96,64},{33,1},{65,33},{97,65},{34,2},{66,34},{98,6... | collective-permute-start | bytes 983048 | tf_op jit(solution)/shard_map/ppermute | solution.py:28
  135.3 9.7 %collective-permute-start.8 = (f32[40,8,1,128]{3,2,1,0:T(1,128)}, f32[40,8,1,128]{3,2,1,0:T(1,128)S(1)}, u32[]{:S(2)}, u32[]{:S(2)}) collective-permute-start(f32[40,8,1,128]{3,2,1,0:T(1,128)} %get-tuple-element.13), channel_id=1, source_target_pairs={{0,8},{8,16},{16,24},{1,9},{9,17},{17,25},{2,10},{10,18},{18,26},{... | collective-permute-start | bytes 491528 | tf_op jit(solution)/shard_map/ppermute | solution.py:27
  138.5 7.0 %copy-start.7 = (f32[8,16,128]{2,1,0:T(8,128)S(1)}, f32[8,16,128]{2,1,0:T(8,128)}, u32[]{:S(2)}) copy-start(f32[8,16,128]{2,1,0:T(8,128)} %get-tuple-element.38) | copy-start | bytes 196612
  138.5 7.0 %copy-start.9 = (f32[8,16,128]{2,1,0:T(8,128)S(1)}, f32[8,16,128]{2,1,0:T(8,128)}, u32[]{:S(2)}) copy-start(f32[8,16,128]{2,1,0:T(8,128)} %get-tuple-element.39) | copy-start | bytes 196612
  138.5 7.0 %copy-start.11 = (f32[8,16,128]{2,1,0:T(8,128)S(1)}, f32[8,16,128]{2,1,0:T(8,128)}, u32[]{:S(2)}) copy-start(f32[8,16,128]{2,1,0:T(8,128)} %get-tuple-element.40) | copy-start | bytes 196612
  138.5 7.0 %copy-start.13 = (f32[8,16,128]{2,1,0:T(8,128)S(1)}, f32[8,16,128]{2,1,0:T(8,128)}, u32[]{:S(2)}) copy-start(f32[8,16,128]{2,1,0:T(8,128)} %get-tuple-element.41) | copy-start | bytes 196612
  138.5 7.0 %copy-start.15 = (f32[8,16,128]{2,1,0:T(8,128)S(1)}, f32[8,16,128]{2,1,0:T(8,128)}, u32[]{:S(2)}) copy-start(f32[8,16,128]{2,1,0:T(8,128)} %get-tuple-element.42) | copy-start | bytes 196612
  138.5 7.0 %collective-permute-start.9 = (f32[40,8,1,128]{3,2,1,0:T(1,128)}, f32[40,8,1,128]{3,2,1,0:T(1,128)}, u32[]{:S(2)}, u32[]{:S(2)}) collective-permute-start(f32[40,8,1,128]{3,2,1,0:T(1,128)} %get-tuple-element.14), channel_id=1, source_target_pairs={{8,0},{16,8},{24,16},{9,1},{17,9},{25,17},{10,2},{18,10},{26,18},{... | collective-permute-start | bytes 491528 | tf_op jit(solution)/shard_map/ppermute | solution.py:28
  171.9 15.4 %copy-start.24 = (f32[100]{0:T(128)S(1)}, f32[100]{0:T(128)}, u32[]{:S(2)}) copy-start(f32[100]{0:T(128)} %param.20) | copy-start | bytes 1204
  171.9 39.9 %all-to-all-start = ((f32[23,128,128]{2,0,1:T(8,128)}), f32[23,128,128]{2,0,1:T(8,128)}, u32[]{:S(2)}, u32[]{:S(2)}) async-start(f32[23,128,128]{2,0,1:T(8,128)} %scatter_fusion), calls=%async_computation | async-start | bytes 3145728 | tf_op jit(solution)/shard_map/all_to_all | solution.py:162
  230.6 30.1 %all-to-all-start.2 = ((f32[23,128,128]{2,0,1:T(8,128)}), f32[23,128,128]{2,0,1:T(8,128)}, u32[]{:S(2)}, u32[]{:S(2)}) async-start(f32[23,128,128]{2,0,1:T(8,128)} %scatter_fusion.1), calls=%async_computation.2 | async-start | bytes 3145728 | tf_op jit(solution)/shard_map/all_to_all | solution.py:172
  236.0 29.6 %copy-start.4 = (f32[40,8,16,128]{3,2,1,0:T(8,128)S(1)}, f32[40,8,16,128]{3,2,1,0:T(8,128)}, u32[]{:S(2)}) copy-start(f32[40,8,16,128]{3,2,1,0:T(8,128)} %copy-done.3) | copy-start | bytes 7864324
  (14 other events, 30.6 us)
where the time goes:
time: 271 us; the launch traced here: 269 us
  local copies, waits for them, and re-layouts  82.5 us (30%)
  starting transfers between devices  65.6 us (24%)
  waiting for transfers between devices  43.4 us (16%)
  other arithmetic  35.1 us (13%)
  blocking collectives  23.8 us (9%)
  between operations  12.5 us (5%)
  matrix products  5.51 us (2%)
    all_to_all x1, waiting for transfers between devices, body(): lax.all_to_all(replies, GX_GY_GZ, split_axis=1, concat_axis=1, tiled=True)  24.7 us
    unnamed x4, blocking collectives  23.8 us
    add x2, other arithmetic, advance(): result + diffuse * (up_cells[direction] + down_cells[direction] - 2.0 * f...  18.3 us
    all_to_all x1, waiting for transfers between devices, body(): lax.all_to_all(outgoing, GX_GY_GZ, split_axis=1, concat_axis=1, tiled=True)  15.9 us
    slice x4, local copies, waits for them, and re-layouts, advance(): below_face = passed_along(fields[:, :, :, -1:], GZ, 1)  15.9 us
    ppermute x4, starting transfers between devices, extended(): lax.ppermute(last, axis, up)  15.5 us
    all_to_all x1, starting transfers between devices, body(): lax.all_to_all(outgoing, GX_GY_GZ, split_axis=1, concat_axis=1, tiled=True)  15.4 us
    scatter x1, local copies, waits for them, and re-layouts, body(): outgoing = jnp.zeros((SPECIES + 1, total_slots, CZ), jnp.float32).at[:, p...  14.2 us
  transfers between devices with their start and end apart: 15, of which 4 were waited for; matrix products, arithmetic and copies ran while one was open for 35% of the time, Pallas kernels for 0%

commit v1 on v0

v1 whole, which is shorter than its diff:
```python
import functools

import jax
import jax.numpy as jnp
from jax import lax
from jax.experimental import pallas as pl
from jax.experimental.pallas import tpu as pltpu
from jax.sharding import PartitionSpec as P

FIELDS = 40
SPECIES = 22
REACTIONS = 100
SUB = 4
CX = 8
CY = 16
CZ = 128
ROWS = CX * CY
GROUP = 8
STEPS = FIELDS // GROUP
BATCH = 8
COURANT = 0.15
CHEM_STEP = 0.25
LOG2E = 1.4426950408889634
AXES = ("gx", "gy", "gz")


def place(axis):
    index = lax.axis_index(axis)
    even = lax.rem(index, 2) == 0
    return even, index > 0, index < lax.axis_size(axis) - 1


def swapped(value, axis, start):
    size = lax.axis_size(axis)
    pairs = []
    for low in range(start, size, 2):
        high = (low + 1) % size
        pairs += [(low, high), (high, low)]
    return lax.ppermute(value, axis, pairs)


def pick_faces(step, block, sends, columns, turned):
    xs0, xs1, ys0, ys1, zs0, zs1 = sends
    xeven, _, _ = place("gx")
    yeven, _, _ = place("gy")
    zeven, _, _ = place("gz")
    high_x = pl.multiple_of(jnp.where(xeven, (CX - 1) * CY, 0), CY)
    low_x = pl.multiple_of(jnp.where(xeven, 0, (CX - 1) * CY), CY)
    high_y = jnp.where(yeven, CY - 1, 0)
    low_y = jnp.where(yeven, 0, CY - 1)
    for f in range(GROUP):
        xs0[f] = block[f, pl.ds(high_x, CY), :]
        xs1[f] = block[f, pl.ds(low_x, CY), :]
        ys0[f] = block[f, pl.ds(high_y, CX, stride=CY), :]
        ys1[f] = block[f, pl.ds(low_y, CX, stride=CY), :]
    lane = lax.broadcasted_iota(jnp.int32, (8, CZ), 1)
    first = step * (2 * GROUP)
    for r in range(0, ROWS, 8):
        total = columns[r : r + 8, :]
        for f in range(GROUP):
            moved = pltpu.roll(block[f, r : r + 8, :], first + 2 * f + 1, 1)
            here = lane - first
            total = jnp.where((here >= 2 * f) & (here < 2 * f + 2), moved, total)
        columns[r : r + 8, :] = total

    @pl.when(step == STEPS - 1)
    def _():
        turned[...] = columns[...].T
        highs = turned[pl.ds(0, FIELDS, stride=2), :]
        lows = turned[pl.ds(1, FIELDS, stride=2), :]
        zs0[...] = jnp.where(zeven, highs, lows)
        zs1[...] = jnp.where(zeven, lows, highs)


def faces_kernel(fields, xs0, xs1, ys0, ys1, zs0, zs1, columns, turned):
    step = pl.program_id(0)

    @pl.when(step == 0)
    def _():
        columns[...] = jnp.zeros_like(columns)

    pick_faces(step, fields, (xs0, xs1, ys0, ys1, zs0, zs1), columns, turned)


def set_up(velocity, halos, weights, columns, turned):
    zh0, zh1 = halos
    for r in range(0, ROWS, 8):
        rest = jnp.ones((8, CZ), jnp.float32)
        for a in range(3):
            speed = velocity[a, r : r + 8, :]
            below = COURANT * jnp.maximum(speed, 0.0)
            above = -COURANT * jnp.minimum(speed, 0.0)
            weights[2 * a, r : r + 8, :] = below
            weights[2 * a + 1, r : r + 8, :] = above
            rest = rest - (below + above)
        weights[6, r : r + 8, :] = rest
    zeven, has_low, has_high = place("gz")
    columns[...] = jnp.zeros_like(columns)
    first, second = zh0[...], zh1[...]
    high = jnp.where(has_high, jnp.where(zeven, first, second), 0.0)
    low = jnp.where(has_low, jnp.where(zeven, second, first), 0.0)
    columns[pl.ds(0, FIELDS, stride=2), :] = high
    columns[pl.ds(1, FIELDS, stride=2), :] = low
    turned[...] = columns[...].T


def move_group(step, block, source, halos, diffusivity, weights, turned, result, base):
    xh0, xh1, yh0, yh1 = halos
    xeven, x_low, x_high = place("gx")
    yeven, y_low, y_high = place("gy")
    row = lax.broadcasted_iota(jnp.int32, (CY, CZ), 0)
    lane = lax.broadcasted_iota(jnp.int32, (CY, CZ), 1)
    diffuse = [diffusivity[step * GROUP + f] for f in range(GROUP)]
    for x in range(CX):
        here = slice(x * CY, (x + 1) * CY)
        share = [weights[k, here, :] for k in range(7)]
        edge = turned[here, :]
        for f in range(GROUP):
            cell = block[f, here, :]
            if x > 0:
                xm = block[f, (x - 1) * CY : x * CY, :]
            else:
                xm = jnp.where(x_low, jnp.where(xeven, xh1[f], xh0[f]), 0.0)
            if x < CX - 1:
                xp = block[f, (x + 1) * CY : (x + 2) * CY, :]
            else:
                xp = jnp.where(x_high, jnp.where(xeven, xh0[f], xh1[f]), 0.0)
            y0 = yh0[f, x : x + 1, :]
            y1 = yh1[f, x : x + 1, :]
            y_below = jnp.where(y_low, jnp.where(yeven, y1, y0), 0.0)
            y_above = jnp.where(y_high, jnp.where(yeven, y0, y1), 0.0)
            ym = jnp.where(row == 0, y_below, pltpu.roll(cell, 1, 0))
            yp = jnp.where(row == CY - 1, y_above, pltpu.roll(cell, CY - 1, 0))
            halo = pltpu.roll(edge, CZ - 1 - 2 * f - step * (2 * GROUP), 1)
            zm = jnp.where(lane == 0, halo, pltpu.roll(cell, 1, 1))
            zp = jnp.where(lane == CZ - 1, halo, pltpu.roll(cell, CZ - 1, 1))
            around = (xm + xp) + (ym + yp) + (zm + zp)
            carried = (
                (share[0] * xm + share[1] * xp)
                + (share[2] * ym + share[3] * yp)
                + (share[4] * zm + share[5] * zp)
            )
            kept = cell * (share[6] - 6.0 * diffuse[f])
            result[base + f, here, :] = (kept + source[f, here, :]) + (
                carried + diffuse[f] * around
            )


def first_kernel(
    diffusivity, fields, source, velocity, xh0, xh1, yh0, yh1, zh0, zh1,
    moved, xs0, xs1, ys0, ys1, zs0, zs1, weights, columns, turned, faces, across,
):
    step = pl.program_id(0)

    @pl.when(step == 0)
    def _():
        set_up(velocity, (zh0, zh1), weights, columns, turned)
        faces[...] = jnp.zeros_like(faces)

    move_group(
        step, fields, source, (xh0, xh1, yh0, yh1), diffusivity, weights, turned, moved, 0
    )
    pick_faces(step, moved, (xs0, xs1, ys0, ys1, zs0, zs1), faces, across)


def react(state, counts, mechanism, prefactor, activation, heat_release, sums):
    taken_a, taken_b, made_c, made_d = sums
    for s in range(SPECIES):
        for part in sums:
            part[s] = jnp.zeros((ROWS, CZ), jnp.float32)

    def substep(number, carry):
        for base in range(0, ROWS, 8 * BATCH):
            rows = [slice(base + 8 * v, base + 8 * v + 8) for v in range(BATCH)]
            cold = [-LOG2E / state[SPECIES, r, :] for r in rows]

            def reaction(j, heats):
                a, b = mechanism[0, j], mechanism[1, j]
                c, d = mechanism[2, j], mechanism[3, j]
                strength, barrier, heat = prefactor[j], activation[j], heat_release[j]
                rates = []
                for v in range(BATCH):
                    rate = strength * jnp.exp2(barrier * cold[v])
                    rates.append(rate * (state[a, rows[v], :] * state[b, rows[v], :]))
                for part, index in ((taken_a, a), (taken_b, b), (made_c, c), (made_d, d)):
                    old = [part[index, rows[v], :] for v in range(BATCH)]
                    for v in range(BATCH):
                        part[index, rows[v], :] = old[v] + rates[v]
                return tuple(heats[v] + heat * rates[v] for v in range(BATCH))

            nothing = tuple(jnp.zeros((8, CZ), jnp.float32) for _ in range(BATCH))
            heats = lax.fori_loop(0, REACTIONS, reaction, nothing, unroll=2)

            for v in range(BATCH):
                many = counts[rows[v], :]
                live = many > number.astype(jnp.float32)
                width = CHEM_STEP / jnp.maximum(many, 1.0)
                old = state[SPECIES, rows[v], :]
                state[SPECIES, rows[v], :] = jnp.where(live, old + width * heats[v], old)

            def species(s, carry):
                empty = jnp.zeros((8, CZ), jnp.float32)
                for v in range(BATCH):
                    many = counts[rows[v], :]
                    live = many > number.astype(jnp.float32)
                    width = CHEM_STEP / jnp.maximum(many, 1.0)
                    old = state[s, rows[v], :]
                    lost = width * (taken_a[s, rows[v], :] + taken_b[s, rows[v], :])
                    gained = width * (made_c[s, rows[v], :] + made_d[s, rows[v], :])
                    new = old * ((old + gained) / (old + lost))
                    state[s, rows[v], :] = jnp.where(live, new, old)
                    for part in sums:
                        part[s, rows[v], :] = empty
                return carry

            lax.fori_loop(0, SPECIES, species, 0)
        return carry

    lax.fori_loop(0, SUB, substep, 0)


def second_kernel(
    diffusivity, mechanism, prefactor, activation, heat_release,
    fields, source, velocity, counts, xh0, xh1, yh0, yh1, zh0, zh1,
    out, weights, columns, turned, state, sum_a, sum_b, sum_c, sum_d, sems,
):
    step = pl.program_id(0)

    def leaving(group):
        part = pl.ds(group * GROUP, GROUP)
        return pltpu.make_async_copy(state.at[part], out.at[part], sems.at[group])

    @pl.when(step == 0)
    def _():
        set_up(velocity, (zh0, zh1), weights, columns, turned)

    move_group(
        step, fields, source, (xh0, xh1, yh0, yh1), diffusivity, weights, turned, state,
        step * GROUP,
    )

    @pl.when(step == STEPS - 1)
    def _():
        for group in range(3, STEPS):
            leaving(group).start()
        react(
            state, counts, mechanism, prefactor, activation, heat_release,
            (sum_a, sum_b, sum_c, sum_d),
        )
        for group in range(3):
            leaving(group).start()
        for group in range(STEPS):
            leaving(group).wait()


def group_spec(*tail):
    return pl.BlockSpec((GROUP,) + tail, lambda g: (g,) + (0,) * len(tail))


def whole_spec(*shape):
    return pl.BlockSpec(shape, lambda g: (0,) * len(shape))


SCALARS = pl.BlockSpec(memory_space=pltpu.SMEM)
HALO_SPECS = [
    group_spec(CY, CZ), group_spec(CY, CZ), group_spec(CX, CZ), group_spec(CX, CZ),
    whole_spec(FIELDS, CZ), whole_spec(FIELDS, CZ),
]
HALO_SHAPES = [
    jax.ShapeDtypeStruct(shape, jnp.float32)
    for shape in (
        (FIELDS, CY, CZ), (FIELDS, CY, CZ), (FIELDS, CX, CZ), (FIELDS, CX, CZ),
        (FIELDS, CZ), (FIELDS, CZ),
    )
]
SQUARE = pltpu.VMEM((ROWS, CZ), jnp.float32)
WEIGHTS = pltpu.VMEM((7, ROWS, CZ), jnp.float32)
PARAMS = pltpu.CompilerParams(dimension_semantics=("arbitrary",))


def exchanged(sends):
    got = []
    for k, axis in enumerate(AXES):
        got += [swapped(sends[2 * k], axis, 0), swapped(sends[2 * k + 1], axis, 1)]
    return got


def body(
    fields, source, velocity, diffusivity, reacting, counts, mechanism, prefactor, activation,
    heat_release,
):
    fields = fields.reshape(FIELDS, ROWS, CZ)
    source = source.reshape(FIELDS, ROWS, CZ)
    velocity = velocity.reshape(3, ROWS, CZ)
    many = jnp.where(reacting == 1, counts, 0).astype(jnp.float32)
    many = jnp.broadcast_to(many, (CX, CY, CZ)).reshape(ROWS, CZ)

    sends = pl.pallas_call(
        faces_kernel,
        grid=(STEPS,),
        in_specs=[group_spec(ROWS, CZ)],
        out_specs=HALO_SPECS,
        out_shape=HALO_SHAPES,
        scratch_shapes=[SQUARE, SQUARE],
        compiler_params=PARAMS,
        name="faces",
    )(fields)
    halos = exchanged(sends)
    moved, *sends = pl.pallas_call(
        first_kernel,
        grid=(STEPS,),
        in_specs=[SCALARS, group_spec(ROWS, CZ), group_spec(ROWS, CZ), whole_spec(3, ROWS, CZ)]
        + HALO_SPECS,
        out_specs=[group_spec(ROWS, CZ)] + HALO_SPECS,
        out_shape=[jax.ShapeDtypeStruct((FIELDS, ROWS, CZ), jnp.float32)] + HALO_SHAPES,
        scratch_shapes=[WEIGHTS, SQUARE, SQUARE, SQUARE, SQUARE],
        compiler_params=PARAMS,
        name="first",
    )(diffusivity, fields, source, velocity, *halos)
    halos = exchanged(sends)
    sums = [pltpu.VMEM((SPECIES, ROWS, CZ), jnp.float32)] * 4
    out = pl.pallas_call(
        second_kernel,
        grid=(STEPS,),
        in_specs=[SCALARS] * 5
        + [group_spec(ROWS, CZ), group_spec(ROWS, CZ), whole_spec(3, ROWS, CZ)]
        + [whole_spec(ROWS, CZ)]
        + HALO_SPECS,
        out_specs=pl.BlockSpec(memory_space=pl.ANY),
        out_shape=jax.ShapeDtypeStruct((FIELDS, ROWS, CZ), jnp.float32),
        scratch_shapes=[WEIGHTS, SQUARE, SQUARE, pltpu.VMEM((FIELDS, ROWS, CZ), jnp.float32)]
        + sums
        + [pltpu.SemaphoreType.DMA((STEPS,))],
        compiler_params=PARAMS,
        name="second",
    )(
        diffusivity, mechanism, prefactor, activation, heat_release,
        moved, source, velocity, many, *halos,
    )
    return out.reshape(FIELDS, CX, CY, CZ)


def solution(mesh):
    grid = P(None, "gx", "gy", "gz")
    placed = (
        grid, grid, grid, P(), P("gx", "gy", "gz"), P("gx", "gy", "gz"), P(), P(), P(), P(),
    )
    return jax.shard_map(body, mesh=mesh, in_specs=placed, out_specs=grid, check_vma=False)
```

time: 271 us -> 69.2 us (0.26)
  local copies, waits for them, and re-layouts: 82.5 us -> 1.89 us
  starting transfers between devices: 65.6 us -> 19 us
  Pallas kernels: 0 us -> 40.6 us
  waiting for transfers between devices: 43.4 us -> 6.27 us
  other arithmetic: 35.1 us -> 0.02 us
  blocking collectives: 23.8 us -> 0 us
  between operations: 12.5 us -> 0.14 us
  matrix products: 5.51 us -> 0 us
    pallas_call x0 -> x3, Pallas kernels: none -> 40.6 us  [the longest x1 27.8 us: body(): pl.pallas_call(second_kernel, grid=(STEPS,), in_specs=[SCALARS] * 5 + [gr...]
    all_to_all x3 -> x0, waiting for transfers between devices: 40.6 us -> none  [the longest x1 24.7 us: body(): lax.all_to_all(replies, GX_GY_GZ, split_axis=1, concat_axis=1, tiled=True)]
    slice x29 -> x0, local copies, waits for them, and re-layouts: 38.4 us -> none  [the longest x4 15.9 us: advance(): below_face = passed_along(fields[:, :, :, -1:], GZ, 1)]
    all_to_all x3 -> x0, starting transfers between devices: 31.6 us -> none  [the longest x1 15.4 us: body(): lax.all_to_all(outgoing, GX_GY_GZ, split_axis=1, concat_axis=1, tiled=True)]
    unnamed x4 -> x0, blocking collectives: 23.8 us -> none
    add x7 -> x0, other arithmetic: 18.6 us -> none  [the longest x2 18.3 us: advance(): result + diffuse * (up_cells[direction] + down_cells[direction] - 2.0 * f...]
    scatter x3 -> x0, local copies, waits for them, and re-layouts: 17.6 us -> none  [the longest x1 14.2 us: body(): outgoing = jnp.zeros((SPECIES + 1, total_slots, CZ), jnp.float32).at[:, p...]
    ppermute x12, starting transfers between devices: 34 us -> 19 us  [swapped(): return lax.ppermute(value, axis, pairs)]
  transfers between devices with their start and end apart: 15 -> 12, of which waited for: 4 -> 4; matrix products, arithmetic and copies ran while one was open for 35% -> 0% of each run, Pallas kernels for 0% -> 0%
where the time goes in v1:
time: 69.2 us; the launch traced here: 68 us
  Pallas kernels  40.6 us (59%)
  starting transfers between devices  19 us (27%)
  waiting for transfers between devices  6.27 us (9%)
  local copies, waits for them, and re-layouts  1.89 us (3%)
    pallas_call x1, Pallas kernels, body(): pl.pallas_call(second_kernel, grid=(STEPS,), in_specs=[SCALARS] * 5 + [gr...  27.8 us
    ppermute x12, starting transfers between devices, swapped(): return lax.ppermute(value, axis, pairs)  19 us
    pallas_call x1, Pallas kernels, body(): pl.pallas_call(first_kernel, grid=(STEPS,), in_specs=[SCALARS, group_spec...  8.06 us
    ppermute x12, waiting for transfers between devices, swapped(): return lax.ppermute(value, axis, pairs)  6.27 us
    pallas_call x1, Pallas kernels, body(): pl.pallas_call(faces_kernel, grid=(STEPS,), in_specs=[group_spec(ROWS, CZ...  4.76 us
  transfers between devices with their start and end apart: 12, of which 4 were waited for; matrix products, arithmetic and copies ran while one was open for 0% of the time, Pallas kernels for 0%

profile of v1, /device:TPU:1, one launch (start us, length us, event | category | flops | bytes accessed | tf_op | source)
XLA Modules:
  0.0 68.0 jit_solution(346055548046973056)
XLA Ops:
  0.0 4.8 %faces.1 = (f32[40,16,128]{2,1,0:T(8,128)}, f32[40,16,128]{2,1,0:T(8,128)}, f32[40,8,128]{2,1,0:T(8,128)}, f32[40,8,128]{2,1,0:T(8,128)}, f32[40,128]{1,0:T(8,128)}, /*index=5*/f32[40,128]{1,0:T(8,128)}) custom-call(f32[40,128,128]{2,1,0:T(8,128)} %bitcast.6), custom_call_target="tpu_custom_call" | custom-call | tf_op jit(solution)/shard_map/faces/pallas_call | solution.py:298
  4.8 2.5 %collective-permute-start = (f32[40,16,128]{2,1,0:T(8,128)}, f32[40,16,128]{2,1,0:T(8,128)S(1)}, u32[]{:S(2)}, u32[]{:S(2)}) collective-permute-start(f32[40,16,128]{2,1,0:T(8,128)} %get-tuple-element.18), channel_id=1, source_target_pairs={{0,32},{32,0},{64,96},{96,64},{1,33},{33,1},{65,97},{97,65},{2,34}... | collective-permute-start | bytes 983048 | tf_op jit(solution)/shard_map/ppermute | solution.py:39
  7.3 2.2 %collective-permute-start.1 = (f32[40,16,128]{2,1,0:T(8,128)}, f32[40,16,128]{2,1,0:T(8,128)S(1)}, u32[]{:S(2)}, u32[]{:S(2)}) collective-permute-start(f32[40,16,128]{2,1,0:T(8,128)} %get-tuple-element.19), channel_id=1, source_target_pairs={{32,64},{64,32},{96,0},{0,96},{33,65},{65,33},{97,1},{1,97},{34,66... | collective-permute-start | bytes 983048 | tf_op jit(solution)/shard_map/ppermute | solution.py:39
  9.5 1.3 %collective-permute-start.2 = (f32[40,8,128]{2,1,0:T(8,128)}, f32[40,8,128]{2,1,0:T(8,128)S(1)}, u32[]{:S(2)}, u32[]{:S(2)}) collective-permute-start(f32[40,8,128]{2,1,0:T(8,128)} %get-tuple-element.20), channel_id=1, source_target_pairs={{0,8},{8,0},{16,24},{24,16},{1,9},{9,1},{17,25},{25,17},{2,10},{10... | collective-permute-start | bytes 491528 | tf_op jit(solution)/shard_map/ppermute | solution.py:39
  10.9 1.9 %collective-permute-start.3 = (f32[40,8,128]{2,1,0:T(8,128)}, f32[40,8,128]{2,1,0:T(8,128)S(1)}, u32[]{:S(2)}, u32[]{:S(2)}) collective-permute-start(f32[40,8,128]{2,1,0:T(8,128)} %get-tuple-element.21), channel_id=1, source_target_pairs={{8,16},{16,8},{24,0},{0,24},{9,17},{17,9},{25,1},{1,25},{10,18},{1... | collective-permute-start | bytes 491528 | tf_op jit(solution)/shard_map/ppermute | solution.py:39
  12.7 1.8 %collective-permute-start.4 = (f32[40,128]{1,0:T(8,128)}, f32[40,128]{1,0:T(8,128)S(1)}, u32[]{:S(2)}, u32[]{:S(2)}) collective-permute-start(f32[40,128]{1,0:T(8,128)} %get-tuple-element.22), channel_id=1, source_target_pairs={{0,1},{1,0},{2,3},{3,2},{4,5},{5,4},{6,7},{7,6},{8,9},{9,8},{10,11... | collective-permute-start | bytes 61448 | tf_op jit(solution)/shard_map/ppermute | solution.py:39
  14.5 1.1 %collective-permute-done.4.zh0 = f32[40,128]{1,0:T(8,128)S(1)} collective-permute-done((f32[40,128]{1,0:T(8,128)}, f32[40,128]{1,0:T(8,128)S(1)}, u32[]{:S(2)}, u32[]{:S(2)}) %collective-permute-start.4) | collective-permute-done | bytes 20512 | tf_op jit(solution)/shard_map/ppermute | solution.py:39
  15.6 1.4 %collective-permute-start.5 = (f32[40,128]{1,0:T(8,128)}, f32[40,128]{1,0:T(8,128)S(1)}, u32[]{:S(2)}, u32[]{:S(2)}) collective-permute-start(f32[40,128]{1,0:T(8,128)} %get-tuple-element.23), channel_id=1, source_target_pairs={{1,2},{2,1},{3,4},{4,3},{5,6},{6,5},{7,0},{0,7},{9,10},{10,9},{11,... | collective-permute-start | bytes 61448 | tf_op jit(solution)/shard_map/ppermute | solution.py:39
  17.0 2.0 %collective-permute-done.5.zh1 = f32[40,128]{1,0:T(8,128)S(1)} collective-permute-done((f32[40,128]{1,0:T(8,128)}, f32[40,128]{1,0:T(8,128)S(1)}, u32[]{:S(2)}, u32[]{:S(2)}) %collective-permute-start.5) | collective-permute-done | bytes 20512 | tf_op jit(solution)/shard_map/ppermute | solution.py:39
  19.0 0.0 collective-permute-done.2.yh0
  19.0 0.0 collective-permute-done.3.yh1
  19.0 0.0 collective-permute-done.xh0
  19.1 0.0 copy-start
  19.1 0.0 collective-permute-done.1.xh1
  19.1 0.5 copy-done.11
  19.6 0.1 copy-done.4
  19.7 0.1 copy-done.5
  19.7 0.1 copy-done
  19.9 0.1 copy-done.2
  20.0 8.1 %first.1 = (f32[40,128,128]{2,1,0:T(8,128)}, f32[40,16,128]{2,1,0:T(8,128)}, f32[40,16,128]{2,1,0:T(8,128)}, f32[40,8,128]{2,1,0:T(8,128)}, f32[40,8,128]{2,1,0:...) custom-call(f32[40]{0:T(128)} %diffusivity.3, f32[40,128,128]{2,1,0:T(8,128)} %bitcast.7, f32[40,128,128]{2,1,0:T(8,128)} %bitcast.4, ...), custom_call_target="tpu_custom_call" | custom-call | tf_op jit(solution)/shard_map/first/pallas_call | solution.py:309
  28.0 0.8 %collective-permute-start.6 = (f32[40,16,128]{2,1,0:T(8,128)}, f32[40,16,128]{2,1,0:T(8,128)S(1)}, u32[]{:S(2)}, u32[]{:S(2)}) collective-permute-start(f32[40,16,128]{2,1,0:T(8,128)} %get-tuple-element.25), channel_id=1, source_target_pairs={{0,32},{32,0},{64,96},{96,64},{1,33},{33,1},{65,97},{97,65},{2,34}... | collective-permute-start | bytes 983048 | tf_op jit(solution)/shard_map/ppermute | solution.py:39
  28.8 0.6 collective-permute-start.7
  29.5 0.4 collective-permute-start.8
  29.9 1.6 %collective-permute-start.9 = (f32[40,8,128]{2,1,0:T(8,128)}, f32[40,8,128]{2,1,0:T(8,128)S(1)}, u32[]{:S(2)}, u32[]{:S(2)}) collective-permute-start(f32[40,8,128]{2,1,0:T(8,128)} %get-tuple-element.28), channel_id=1, source_target_pairs={{8,16},{16,8},{24,0},{0,24},{9,17},{17,9},{25,1},{1,25},{10,18},{1... | collective-permute-start | bytes 491528 | tf_op jit(solution)/shard_map/ppermute | solution.py:39
  31.5 2.9 %collective-permute-start.10 = (f32[40,128]{1,0:T(8,128)}, f32[40,128]{1,0:T(8,128)S(1)}, u32[]{:S(2)}, u32[]{:S(2)}) collective-permute-start(f32[40,128]{1,0:T(8,128)} %get-tuple-element.29), channel_id=1, source_target_pairs={{0,1},{1,0},{2,3},{3,2},{4,5},{5,4},{6,7},{7,6},{8,9},{9,8},{10,11... | collective-permute-start | bytes 61448 | tf_op jit(solution)/shard_map/ppermute | solution.py:39
  34.4 1.1 %collective-permute-done.10.zh0 = f32[40,128]{1,0:T(8,128)S(1)} collective-permute-done((f32[40,128]{1,0:T(8,128)}, f32[40,128]{1,0:T(8,128)S(1)}, u32[]{:S(2)}, u32[]{:S(2)}) %collective-permute-start.10) | collective-permute-done | bytes 20512 | tf_op jit(solution)/shard_map/ppermute | solution.py:39
  35.5 1.4 %collective-permute-start.11 = (f32[40,128]{1,0:T(8,128)}, f32[40,128]{1,0:T(8,128)S(1)}, u32[]{:S(2)}, u32[]{:S(2)}) collective-permute-start(f32[40,128]{1,0:T(8,128)} %get-tuple-element.30), channel_id=1, source_target_pairs={{1,2},{2,1},{3,4},{4,3},{5,6},{6,5},{7,0},{0,7},{9,10},{10,9},{11,... | collective-permute-start | bytes 61448 | tf_op jit(solution)/shard_map/ppermute | solution.py:39
  36.9 0.1 broadcast_in_dim.12
  37.0 2.2 %collective-permute-done.11.zh1 = f32[40,128]{1,0:T(8,128)S(1)} collective-permute-done((f32[40,128]{1,0:T(8,128)}, f32[40,128]{1,0:T(8,128)S(1)}, u32[]{:S(2)}, u32[]{:S(2)}) %collective-permute-start.11) | collective-permute-done | bytes 20512 | tf_op jit(solution)/shard_map/ppermute | solution.py:39
  39.2 0.9 %broadcast_in_dim.13.counts = f32[128,128]{1,0:T(8,128)} broadcast(f32[128]{0:T(128)S(1)} %broadcast_in_dim.12), dimensions={0} | broadcast | bytes 66048 | tf_op jit(solution)/shard_map/broadcast_in_dim | solution.py:296
  40.1 0.1 copy-done.3
  40.2 27.8 %second.1 = f32[40,128,128]{2,1,0:T(8,128)} custom-call(f32[40]{0:T(128)} %diffusivity.3, s32[4,100]{1,0:T(4,128)} %mechanism.1, f32[100]{0:T(128)} %prefactor.1, f32[100]{0:T(128)} %activation.1, f32[100]{0:T(128)} %heat_release.1, f32[40,128,128]{2,1,0:T(8,128)} %get-tuple-element.24.fields, f32[40,128,128]{2,1,0:T(8,128)} %bitcast.5, ...), custom_call_target="tpu_custom_call" | custom-call | tf_op jit(solution)/shard_map/second/pallas_call | solution.py:322
  (26 shorter events, 0.1 us)
Async XLA Ops:
  4.8 14.3 %collective-permute-start = (f32[40,16,128]{2,1,0:T(8,128)}, f32[40,16,128]{2,1,0:T(8,128)S(1)}, u32[]{:S(2)}, u32[]{:S(2)}) collective-permute-start(f32[40,16,128]{2,1,0:T(8,128)} %get-tuple-element.18), channel_id=1, source_target_pairs={{0,32},{32,0},{64,96},{96,64},{1,33},{33,1},{65,97},{97,65},{2,34}... | collective-permute-start | bytes 983048 | tf_op jit(solution)/shard_map/ppermute | solution.py:39
  7.3 11.8 %collective-permute-start.1 = (f32[40,16,128]{2,1,0:T(8,128)}, f32[40,16,128]{2,1,0:T(8,128)S(1)}, u32[]{:S(2)}, u32[]{:S(2)}) collective-permute-start(f32[40,16,128]{2,1,0:T(8,128)} %get-tuple-element.19), channel_id=1, source_target_pairs={{32,64},{64,32},{96,0},{0,96},{33,65},{65,33},{97,1},{1,97},{34,66... | collective-permute-start | bytes 983048 | tf_op jit(solution)/shard_map/ppermute | solution.py:39
  9.5 9.5 %collective-permute-start.2 = (f32[40,8,128]{2,1,0:T(8,128)}, f32[40,8,128]{2,1,0:T(8,128)S(1)}, u32[]{:S(2)}, u32[]{:S(2)}) collective-permute-start(f32[40,8,128]{2,1,0:T(8,128)} %get-tuple-element.20), channel_id=1, source_target_pairs={{0,8},{8,0},{16,24},{24,16},{1,9},{9,1},{17,25},{25,17},{2,10},{10... | collective-permute-start | bytes 491528 | tf_op jit(solution)/shard_map/ppermute | solution.py:39
  10.9 8.2 %collective-permute-start.3 = (f32[40,8,128]{2,1,0:T(8,128)}, f32[40,8,128]{2,1,0:T(8,128)S(1)}, u32[]{:S(2)}, u32[]{:S(2)}) collective-permute-start(f32[40,8,128]{2,1,0:T(8,128)} %get-tuple-element.21), channel_id=1, source_target_pairs={{8,16},{16,8},{24,0},{0,24},{9,17},{17,9},{25,1},{1,25},{10,18},{1... | collective-permute-start | bytes 491528 | tf_op jit(solution)/shard_map/ppermute | solution.py:39
  12.7 2.9 %collective-permute-start.4 = (f32[40,128]{1,0:T(8,128)}, f32[40,128]{1,0:T(8,128)S(1)}, u32[]{:S(2)}, u32[]{:S(2)}) collective-permute-start(f32[40,128]{1,0:T(8,128)} %get-tuple-element.22), channel_id=1, source_target_pairs={{0,1},{1,0},{2,3},{3,2},{4,5},{5,4},{6,7},{7,6},{8,9},{9,8},{10,11... | collective-permute-start | bytes 61448 | tf_op jit(solution)/shard_map/ppermute | solution.py:39
  15.6 3.5 %copy-start.10 = (f32[40,128]{1,0:T(8,128)}, f32[40,128]{1,0:T(8,128)S(1)}, u32[]{:S(2)}) copy-start(f32[40,128]{1,0:T(8,128)S(1)} %collective-permute-done.4.zh0) | copy-start | bytes 61444
  15.6 3.4 %collective-permute-start.5 = (f32[40,128]{1,0:T(8,128)}, f32[40,128]{1,0:T(8,128)S(1)}, u32[]{:S(2)}, u32[]{:S(2)}) collective-permute-start(f32[40,128]{1,0:T(8,128)} %get-tuple-element.23), channel_id=1, source_target_pairs={{1,2},{2,1},{3,4},{4,3},{5,6},{6,5},{7,0},{0,7},{9,10},{10,9},{11,... | collective-permute-start | bytes 61448 | tf_op jit(solution)/shard_map/ppermute | solution.py:39
  19.0 0.6 copy-start.11
  19.0 0.7 copy-start.4
  19.0 0.7 %copy-start.5 = (f32[40,8,128]{2,1,0:T(8,128)}, f32[40,8,128]{2,1,0:T(8,128)S(1)}, u32[]{:S(2)}) copy-start(f32[40,8,128]{2,1,0:T(8,128)S(1)} %collective-permute-done.3.yh1) | copy-start | bytes 491524
  19.1 0.8 %copy-start = (f32[40,16,128]{2,1,0:T(8,128)}, f32[40,16,128]{2,1,0:T(8,128)S(1)}, u32[]{:S(2)}) copy-start(f32[40,16,128]{2,1,0:T(8,128)S(1)} %collective-permute-done.xh0) | copy-start | bytes 983044
  19.1 0.9 %copy-start.2 = (f32[40,16,128]{2,1,0:T(8,128)}, f32[40,16,128]{2,1,0:T(8,128)S(1)}, u32[]{:S(2)}) copy-start(f32[40,16,128]{2,1,0:T(8,128)S(1)} %collective-permute-done.1.xh1) | copy-start | bytes 983044
  19.9 17.0 %copy-start.12 = (s32[8,16,1]{1,2,0:T(1,128)S(1)}, s32[8,16,1]{1,2,0:T(1,128)}, u32[]{:S(2)}) copy-start(s32[8,16,1]{1,2,0:T(1,128)} %param.15) | copy-start | bytes 1540
  19.9 17.0 %copy-start.13 = (s32[8,16,1]{1,2,0:T(1,128)S(1)}, s32[8,16,1]{1,2,0:T(1,128)}, u32[]{:S(2)}) copy-start(s32[8,16,1]{1,2,0:T(1,128)} %param.14) | copy-start | bytes 1540
  28.0 11.2 %collective-permute-start.6 = (f32[40,16,128]{2,1,0:T(8,128)}, f32[40,16,128]{2,1,0:T(8,128)S(1)}, u32[]{:S(2)}, u32[]{:S(2)}) collective-permute-start(f32[40,16,128]{2,1,0:T(8,128)} %get-tuple-element.25), channel_id=1, source_target_pairs={{0,32},{32,0},{64,96},{96,64},{1,33},{33,1},{65,97},{97,65},{2,34}... | collective-permute-start | bytes 983048 | tf_op jit(solution)/shard_map/ppermute | solution.py:39
  28.8 10.4 %collective-permute-start.7 = (f32[40,16,128]{2,1,0:T(8,128)}, f32[40,16,128]{2,1,0:T(8,128)S(1)}, u32[]{:S(2)}, u32[]{:S(2)}) collective-permute-start(f32[40,16,128]{2,1,0:T(8,128)} %get-tuple-element.26), channel_id=1, source_target_pairs={{32,64},{64,32},{96,0},{0,96},{33,65},{65,33},{97,1},{1,97},{34,66... | collective-permute-start | bytes 983048 | tf_op jit(solution)/shard_map/ppermute | solution.py:39
  29.5 9.7 %collective-permute-start.8 = (f32[40,8,128]{2,1,0:T(8,128)}, f32[40,8,128]{2,1,0:T(8,128)S(1)}, u32[]{:S(2)}, u32[]{:S(2)}) collective-permute-start(f32[40,8,128]{2,1,0:T(8,128)} %get-tuple-element.27), channel_id=1, source_target_pairs={{0,8},{8,0},{16,24},{24,16},{1,9},{9,1},{17,25},{25,17},{2,10},{10... | collective-permute-start | bytes 491528 | tf_op jit(solution)/shard_map/ppermute | solution.py:39
  29.9 9.3 %collective-permute-start.9 = (f32[40,8,128]{2,1,0:T(8,128)}, f32[40,8,128]{2,1,0:T(8,128)S(1)}, u32[]{:S(2)}, u32[]{:S(2)}) collective-permute-start(f32[40,8,128]{2,1,0:T(8,128)} %get-tuple-element.28), channel_id=1, source_target_pairs={{8,16},{16,8},{24,0},{0,24},{9,17},{17,9},{25,1},{1,25},{10,18},{1... | collective-permute-start | bytes 491528 | tf_op jit(solution)/shard_map/ppermute | solution.py:39
  31.5 4.0 %collective-permute-start.10 = (f32[40,128]{1,0:T(8,128)}, f32[40,128]{1,0:T(8,128)S(1)}, u32[]{:S(2)}, u32[]{:S(2)}) collective-permute-start(f32[40,128]{1,0:T(8,128)} %get-tuple-element.29), channel_id=1, source_target_pairs={{0,1},{1,0},{2,3},{3,2},{4,5},{5,4},{6,7},{7,6},{8,9},{9,8},{10,11... | collective-permute-start | bytes 61448 | tf_op jit(solution)/shard_map/ppermute | solution.py:39
  35.5 4.6 %copy-start.8 = (f32[40,128]{1,0:T(8,128)}, f32[40,128]{1,0:T(8,128)S(1)}, u32[]{:S(2)}) copy-start(f32[40,128]{1,0:T(8,128)S(1)} %collective-permute-done.10.zh0) | copy-start | bytes 61444
  35.5 3.7 %collective-permute-start.11 = (f32[40,128]{1,0:T(8,128)}, f32[40,128]{1,0:T(8,128)S(1)}, u32[]{:S(2)}, u32[]{:S(2)}) collective-permute-start(f32[40,128]{1,0:T(8,128)} %get-tuple-element.30), channel_id=1, source_target_pairs={{1,2},{2,1},{3,4},{4,3},{5,6},{6,5},{7,0},{0,7},{9,10},{10,9},{11,... | collective-permute-start | bytes 61448 | tf_op jit(solution)/shard_map/ppermute | solution.py:39
  39.2 0.9 %copy-start.9 = (f32[40,128]{1,0:T(8,128)}, f32[40,128]{1,0:T(8,128)S(1)}, u32[]{:S(2)}) copy-start(f32[40,128]{1,0:T(8,128)S(1)} %collective-permute-done.11.zh1) | copy-start | bytes 61444
  39.2 0.9 %copy-start.6 = (f32[40,8,128]{2,1,0:T(8,128)}, f32[40,8,128]{2,1,0:T(8,128)S(1)}, u32[]{:S(2)}) copy-start(f32[40,8,128]{2,1,0:T(8,128)S(1)} %collective-permute-done.8.yh0) | copy-start | bytes 491524
  39.2 0.9 %copy-start.7 = (f32[40,8,128]{2,1,0:T(8,128)}, f32[40,8,128]{2,1,0:T(8,128)S(1)}, u32[]{:S(2)}) copy-start(f32[40,8,128]{2,1,0:T(8,128)S(1)} %collective-permute-done.9.yh1) | copy-start | bytes 491524
  39.2 0.9 %copy-start.1 = (f32[40,16,128]{2,1,0:T(8,128)}, f32[40,16,128]{2,1,0:T(8,128)S(1)}, u32[]{:S(2)}) copy-start(f32[40,16,128]{2,1,0:T(8,128)S(1)} %collective-permute-done.6.xh0) | copy-start | bytes 983044
  39.2 0.9 %copy-start.3 = (f32[40,16,128]{2,1,0:T(8,128)}, f32[40,16,128]{2,1,0:T(8,128)S(1)}, u32[]{:S(2)}) copy-start(f32[40,16,128]{2,1,0:T(8,128)S(1)} %collective-permute-done.7.xh1) | copy-start | bytes 983044
